TPU v7x, 32 devices: a whole 2x2x4 slice. The times are simulated.
32 devices in a mesh: grp: 4 (over y, x), seq: 8 (over z, core).
Axes of the slice: x: 2, y: 2, z: 4, core: 2. Of those that a mesh axis runs over, the one named last changes fastest.
Arguments:
- queries: bfloat16 [8, 256, 8192], P('grp', 'seq'), parts along dimension 0, may hold values from -400 to 400
- stretch_keys: bfloat16 [8, 256, 1024], P('grp', 'seq'), parts along dimension 0, may hold values from -6 to 6
- stretch_values: bfloat16 [8, 256, 1024], P('grp', 'seq'), parts along dimension 0, may hold values from -6 to 6
- cache_keys: bfloat16 [8, 512, 1024], P('grp', 'seq'), parts along dimension 0, may hold values from -6 to 6
- cache_values: bfloat16 [8, 512, 1024], P('grp', 'seq'), parts along dimension 0, may hold values from -6 to 6
- prefix_len: int32 [8], P('grp'), parts along dimension 0, may hold values from 16 to 512, as said below
Outputs:
- attention: bfloat16 [8, 256, 8192], P('grp', 'seq'), parts along dimension 0
- prefix_bounds: bfloat16 [8, 32, 2048], P('grp', 'seq'), parts along dimension 0
- stretch_bounds: bfloat16 [8, 16, 2048], P('grp', 'seq'), parts along dimension 0
There are 4 independent parts, one for each index of `grp`. A program takes and returns all parts, laid end to end along the dimension named above; each array names one. Nothing has to cross between parts.
Inputs may be any that keep to these rules, and one draw needn't show every extreme that they name: `prefix_len`: multiples of 16; some sequence of every group has 512.
All inputs are finite; a program needn't handle non-finite values.
Results may differ from a plain program's by a relative error of at most 0.006.
Values may be sent and summed in bfloat16 or wider, within the bound.
A program may use at most 128 MiB of HBM per device.

v0:
```python
import math
import jax
import jax.numpy as jnp
from jax import lax
from jax.sharding import PartitionSpec as P

HQ = 64
HK = 8
DH = 128
PAGE = 16


def pick_block(length):
    for candidate in range(min(length, 512), 0, -1):
        if length % candidate == 0:
            return candidate
    return 1


def online(state, query_rows, query_pos, key_rows, value_rows, key_pos, from_cache, prefix_len):
    seqs, rows, _ = query_rows.shape
    group = HQ // HK
    factor = 1.0 / math.sqrt(DH)
    length = key_rows.shape[1]
    block = pick_block(length)
    steps_count = length // block
    shaped_query = query_rows.reshape(seqs, rows, HK, group, DH)
    key_blocks = jnp.moveaxis(key_rows.reshape(seqs, steps_count, block, HK, DH), 1, 0)
    value_blocks = jnp.moveaxis(value_rows.reshape(seqs, steps_count, block, HK, DH), 1, 0)
    pos_blocks = key_pos.reshape(steps_count, block)
    cache_blocks = from_cache.reshape(steps_count, block)
    top_length = jnp.max(prefix_len)
    top_query = jnp.max(query_pos)

    def one_step(current, pieces):
        key_part, value_part, pos_part, cache_part = pieces

        def compute(carried):
            running_top, running_sum, running_acc = carried
            scores = (
                jnp.einsum(
                    "srhgd,skhd->srhgk", shaped_query, key_part, preferred_element_type=jnp.float32
                )
                * factor
            )
            live = jnp.where(
                cache_part[None, None, :],
                pos_part[None, None, :] < prefix_len[:, None, None],
                pos_part[None, None, :] <= query_pos[None, :, None],
            )
            live = live[:, :, None, None, :]
            new_top = jnp.maximum(running_top, jnp.max(jnp.where(live, scores, -1e30), axis=-1))
            weights = jnp.where(live, jnp.exp(scores - new_top[..., None]), 0.0)
            shrink = jnp.exp(running_top - new_top)
            new_sum = running_sum * shrink + jnp.sum(weights, axis=-1)
            new_acc = running_acc * shrink[..., None] + jnp.einsum(
                "srhgk,skhd->srhgd",
                weights.astype(jnp.bfloat16),
                value_part,
                preferred_element_type=jnp.float32,
            )
            return (new_top, new_sum, new_acc)

        useful = jnp.any(jnp.where(cache_part, pos_part < top_length, pos_part <= top_query))
        return (lax.cond(useful, compute, lambda carried: carried, current), None)

    result, _ = lax.scan(one_step, state, (key_blocks, value_blocks, pos_blocks, cache_blocks))
    return result


def page_bounds(key_rows, live_pages):
    seqs, rows, width = key_rows.shape
    shaped = key_rows.reshape(seqs, rows // PAGE, PAGE, width)
    joined = jnp.concatenate([jnp.min(shaped, axis=2), jnp.max(shaped, axis=2)], axis=2)
    return jnp.where(live_pages[:, :, None], joined, jnp.zeros_like(joined))


def on_device(queries, stretch_keys, stretch_values, cache_keys, cache_values, prefix_len):
    seqs, ch_rows, _ = queries.shape
    pre_rows = cache_keys.shape[1]
    own_index = lax.axis_index("seq")
    group = HQ // HK
    groups = ((queries, own_index * ch_rows + jnp.arange(ch_rows, dtype=jnp.int32)),)
    states = tuple(
        (
            (
                jnp.full((seqs, entry[0].shape[1], HK, group), -1e30, jnp.float32),
                jnp.zeros((seqs, entry[0].shape[1], HK, group), jnp.float32),
                jnp.zeros((seqs, entry[0].shape[1], HK, group, DH), jnp.float32),
            )
            for entry in groups
        )
    )

    def absorb(current, key_rows, value_rows, key_pos, from_cache):
        return tuple(
            (
                online(
                    state, entry[0], entry[1], key_rows, value_rows, key_pos, from_cache, prefix_len
                )
                for state, entry in zip(current, groups)
            )
        )

    old_keys, old_values = (
        lax.all_gather(cache_keys, "seq", axis=1, tiled=True),
        lax.all_gather(cache_values, "seq", axis=1, tiled=True),
    )
    new_keys, new_values = (
        lax.all_gather(stretch_keys, "seq", axis=1, tiled=True),
        lax.all_gather(stretch_values, "seq", axis=1, tiled=True),
    )
    old_count = old_keys.shape[1]
    new_count = new_keys.shape[1]
    states = absorb(
        states,
        old_keys,
        old_values,
        jnp.arange(old_count, dtype=jnp.int32),
        jnp.ones((old_count,), bool),
    )
    states = absorb(
        states,
        new_keys,
        new_values,
        jnp.arange(new_count, dtype=jnp.int32),
        jnp.zeros((new_count,), bool),
    )
    outputs = [
        (state[2] / state[1][..., None])
        .reshape(seqs, state[2].shape[1], HQ * DH)
        .astype(jnp.bfloat16)
        for state in states
    ]
    attention = outputs[0]
    page_index = own_index * (pre_rows // PAGE) + jnp.arange(pre_rows // PAGE, dtype=jnp.int32)
    prefix_live = page_index[None, :] * PAGE < prefix_len[:, None]
    stretch_live = jnp.ones((seqs, ch_rows // PAGE), bool)
    return (
        attention,
        page_bounds(cache_keys, prefix_live),
        page_bounds(stretch_keys, stretch_live),
    )


def solution(mesh):
    return jax.shard_map(
        on_device,
        mesh=mesh,
        in_specs=(
            P("grp", "seq", None),
            P("grp", "seq", None),
            P("grp", "seq", None),
            P("grp", "seq", None),
            P("grp", "seq", None),
            P("grp"),
        ),
        out_specs=(P("grp", "seq", None), P("grp", "seq", None), P("grp", "seq", None)),
        check_vma=False,
    )
```

profile of v0, /device:TPU:0, one launch (start us, length us, event | category | flops | bytes accessed | tf_op | source)
XLA Modules:
  0.0 138.9 jit_solution(6246372038849168881)
XLA Ops:
  10.0 1.5 %copy.52 = bf16[8,8,64,128]{3,2,1,0:T(8,128)(2,1)S(1)} copy(bf16[8,8,64,128]{3,1,2,0:T(8,128)(2,1)} %bitcast.84) | data formatting | bytes 2097152
  12.2 1.3 fusion.28
  14.7 1.3 compare_reduce_fusion
  17.5 1.0 bitcast_reduce_fusion.3
  20.1 21.4 %all-gather.5.cloned.1.call-done = bf16[2,512,1024]{2,1,0:T(8,128)(2,1)} async-done(((bf16[2,64,1024]{2,1,0:T(8,128)(2,1)}), bf16[2,512,1024]{2,1,0:T(8,128)(2,1)}) %all-gather.5.cloned.1.call-update) | async-done | bytes 2097168 | tf_op jit(solution)/shard_map/all_gather | solution.py:106
  41.5 30.2 %all-gather.7.cloned.1.call-done = bf16[2,512,1024]{2,1,0:T(8,128)(2,1)} async-done(((bf16[2,64,1024]{2,1,0:T(8,128)(2,1)}), bf16[2,512,1024]{2,1,0:T(8,128)(2,1)}) %all-gather.7.cloned.1.call-update) | async-done | bytes 2097168 | tf_op jit(solution)/shard_map/all_gather | solution.py:107
  71.7 19.0 %conditional.2 = ((f32[2,32,8,8]{1,3,2,0:T(8,128)S(1)}, f32[2,32,8,8]{1,3,2,0:T(8,128)}, f32[2,32,8,8,128]{4,3,1,2,0:T(8,128)S(1)})) conditional(s32[]{:T(128)} %convert_element_type.24, (f32[2,32,8,8]{1,3,2,0:T(8,128)S(1)}, f32[2,32,8,8]{1,3,2,0:T(8,128)}, f32[2,32,8,8,128]{4,3,1,2,0:T(8,128)S(1)}) %tuple.36, (s32[512]{0:T(512)S(1)}, ...), branch_computations={%region_4.5_spmd, %region_5.8_spmd} | conditional | flops 1091576832 | bytes 68441152 | solution.py:65
  71.8 2.2 %copy.48 = bf16[128,8,8,128]{3,2,1,0:T(8,128)(2,1)S(1)} copy(bf16[128,8,8,128]{3,1,2,0:T(8,128)(2,1)} %bitcast.82) | data formatting | bytes 4194304 | tf_op jit(solution)/shard_map/while/body/eval_jaxpr/cond
  74.1 2.5 %fusion = (f32[2,32,8,8]{1,3,2,0:T(8,128)S(1)}, f32[2,8,512,32,8]{2,3,4,1,0:T(8,128)S(1)}) fusion(pred[2,512]{1,0:T(4,128)(4,1)S(1)} %broadcast_compare_fusion, bf16[2,32,8,8,128]{4,3,2,1,0:T(8,128)(2,1)S(1)} %get-tuple-element.213, bf16[2,512,8,128,1]{3,2,1,0,4:T(8,128)(2,1)S(1)} %bitcast_bitcast_fusion.1), kind=kOutput, calls=%fused_computation.2 | convolution fusion | flops 543158272 | bytes 11551744 | tf_op jit(solution)/shard_map/while/body/eval_jaxpr/cond/branch_1_fun/srhgd,skhd->srhgk/dot_general | solution.py:41
  76.6 3.6 %fusion.3 = (bf16[2,32,8,8,512]{4,1,3,2,0:T(8,128)(2,1)}, f32[2,32,8,8]{1,3,2,0:T(8,128)S(1)}) fusion(f32[2,8,512,32,8]{2,3,4,1,0:T(8,128)S(1)} %get-tuple-element.255, f32[2,32,8,8]{1,3,2,0:T(8,128)S(1)} %max.7, pred[2,512]{1,0:T(4,128)(4,1)S(1)} %broadcast_compare_fusion), kind=kLoop, calls=%fused_computation.5 | loop fusion | flops 10481664 | bytes 12616704 | tf_op jit(solution)/shard_map/while/body/eval_jaxpr/cond/branch_1_fun/convert_element_type | solution.py:58
  80.2 1.5 %multiply_add_fusion = (f32[2,32,8,8]{1,3,2,0:T(8,128)}, f32[2,32,8,8]{1,3,2,0:T(8,128)}) fusion(f32[2,32,8,8]{1,3,2,0:T(8,128)S(1)} %get-tuple-element.253, f32[2,32,8,8]{1,3,2,0:T(8,128)} %get-tuple-element.184, f32[2,32,8,8]{1,3,2,0:T(8,128)S(1)} %get-tuple-element.179, f32[2,32,8,8]{1,3,2,0:T(8,128)S(1)} %max.7), kind=kLoop, calls=%fused_computation.16 | loop fusion | flops 12288 | bytes 98304 | tf_op jit(solution)/shard_map/while/body/eval_jaxpr/cond/branch_1_fun/add | solution.py:55
  82.7 2.2 %copy.49 = bf16[128,8,8,128]{3,2,1,0:T(8,128)(2,1)S(1)} copy(bf16[128,8,8,128]{3,1,2,0:T(8,128)(2,1)} %bitcast.83) | data formatting | bytes 4194304 | tf_op jit(solution)/shard_map/while/body/eval_jaxpr/cond
  85.1 2.1 %copy-done.1 = bf16[2,32,8,8,512]{4,1,3,2,0:T(8,128)(2,1)S(1)} copy-done((bf16[2,32,8,8,512]{4,1,3,2,0:T(8,128)(2,1)S(1)}, bf16[2,32,8,8,512]{4,1,3,2,0:T(8,128)(2,1)}, u32[]{:S(2)}) %copy-start.1) | copy-done | bytes 4194328 | tf_op jit(solution)/shard_map/while/body/eval_jaxpr/cond
  87.2 3.4 %bitcast_add_fusion = f32[2,32,8,8,128]{4,3,1,2,0:T(8,128)S(1)} fusion(f32[2,32,8,8,128]{4,3,1,2,0:T(8,128)S(1)} %get-tuple-element.185, bf16[2,512,8,128,1]{3,2,1,0,4:T(8,128)(2,1)S(1)} %bitcast_bitcast_fusion, bf16[2,32,8,8,512]{4,1,3,2,0:T(8,128)(2,1)S(1)} %copy-done.1, f32[2,32,8,8]{3,1,2,0:T(8,128)S(1)} %copy.20), kind=kOutput, calls=%fused_computation.11 | convolution fusion | flops 537919488 | bytes 10502144 | tf_op jit(solution)/shard_map/while/body/eval_jaxpr/cond/branch_1_fun/srhgk,skhd->srhgd/dot_general | solution.py:56
  90.7 4.3 %all-gather.11.cloned.1.call-done = bf16[2,256,1024]{2,1,0:T(8,128)(2,1)} async-done(((bf16[2,32,1024]{2,1,0:T(8,128)(2,1)}), bf16[2,256,1024]{2,1,0:T(8,128)(2,1)}) %all-gather.11.cloned.1.call-update) | async-done | bytes 1048592 | tf_op jit(solution)/shard_map/all_gather | solution.py:111
  95.0 23.3 %all-gather.9.cloned.1.call-done = bf16[2,256,1024]{2,1,0:T(8,128)(2,1)} async-done(((bf16[2,32,1024]{2,1,0:T(8,128)(2,1)}), bf16[2,256,1024]{2,1,0:T(8,128)(2,1)}) %all-gather.9.cloned.1.call-update) | async-done | bytes 1048592 | tf_op jit(solution)/shard_map/all_gather | solution.py:110
  118.3 10.8 %conditional.3 = ((f32[2,32,8,8]{1,3,2,0:T(8,128)}, f32[2,32,8,8,128]{4,3,1,2,0:T(8,128)S(1)})) conditional(s32[]{:T(128)} %convert_element_type.23, (f32[2,32,8,8]{1,3,2,0:T(8,128)}, f32[2,32,8,8,128]{4,3,1,2,0:T(8,128)S(1)}) %tuple.38, (s32[256]{0:T(256)S(1)}, s32[32]{0:T(128)S(1)}, bf16[2,256,1024]{2,1,0:T(8,128)(2,1)}, ...), branch_computations={%region_8.9_spmd, %region_9.12_spmd.clone} | conditional | flops 546324480 | bytes 41166032 | solution.py:65
  118.4 1.5 %copy.50 = bf16[64,8,8,128]{3,2,1,0:T(8,128)(2,1)S(1)} copy(bf16[64,8,8,128]{3,1,2,0:T(8,128)(2,1)} %bitcast.86) | data formatting | bytes 2097152 | tf_op jit(solution)/shard_map/while/body/eval_jaxpr/cond
  119.9 1.4 fusion.15
  121.3 2.5 %fusion.18 = (bf16[2,32,8,8,256]{4,1,3,2,0:T(8,128)(2,1)}, f32[2,32,8,8]{1,3,2,0:T(8,128)S(1)}) fusion(f32[2,8,256,32,8]{2,3,4,1,0:T(8,128)S(1)} %get-tuple-element.259, f32[2,32,8,8]{1,3,2,0:T(8,128)S(1)} %max.9, pred[32,256]{1,0:T(8,128)(4,1)S(1)} %broadcast_compare_fusion.1), kind=kLoop, calls=%fused_computation.24 | loop fusion | flops 5238784 | bytes 6332416 | tf_op jit(solution)/shard_map/while/body/eval_jaxpr/cond/branch_1_fun/convert_element_type | solution.py:58
  123.8 1.5 %multiply_add_fusion.1 = (f32[2,32,8,8]{1,3,2,0:T(8,128)}, f32[2,32,8,8]{1,3,2,0:T(8,128)S(1)}) fusion(f32[2,32,8,8]{1,3,2,0:T(8,128)S(1)} %get-tuple-element.257, f32[2,32,8,8]{1,3,2,0:T(8,128)} %get-tuple-element.233, f32[2,32,8,8]{1,3,2,0:T(8,128)S(1)} %get-tuple-element.232, f32[2,32,8,8]{1,3,2,0:T(8,128)S(1)} %max.9), kind=kLoop, calls=%fused_computation.35 | loop fusion | flops 12288 | bytes 98304 | tf_op jit(solution)/shard_map/while/body/eval_jaxpr/cond/branch_1_fun/add | solution.py:55
  125.8 1.2 copy-done
  127.0 2.0 %bitcast_add_fusion.1 = f32[2,32,8,8,128]{4,3,1,2,0:T(8,128)S(1)} fusion(f32[2,32,8,8,128]{4,3,1,2,0:T(8,128)S(1)} %get-tuple-element.234, bf16[2,32,8,8,256]{4,1,3,2,0:T(8,128)(2,1)S(1)} %copy-done, bf16[2,256,8,128,1]{3,2,1,0,4:T(8,128)(2,1)S(1)} %bitcast_bitcast_fusion.2, f32[2,32,8,8]{3,1,2,0:T(8,128)S(1)} %copy.43), kind=kOutput, calls=%fused_computation.26 | convolution fusion | flops 269484032 | bytes 7356416 | tf_op jit(solution)/shard_map/while/body/eval_jaxpr/cond/branch_1_fun/srhgk,skhd->srhgd/dot_general | solution.py:56
  131.1 1.3 convert_element_type.26
  (44 shorter events, 10.3 us)
Async XLA Ops:
  7.2 4.4 %copy-start.4 = (s32[2]{0:T(128)S(1)}, s32[2]{0:T(128)}, u32[]{:S(2)}) copy-start(s32[2]{0:T(128)} %param.15) | copy-start | bytes 28
  7.2 34.3 %all-gather.5.cloned.1.call-start = ((), (), s32[]{:S(2)}) async-start(), calls=%async_computation | async-start | bytes 2359296 | tf_op jit(solution)/shard_map/all_gather | solution.py:106
  7.9 63.8 %all-gather.7.cloned.1.call-start = ((), (), s32[]{:S(2)}) async-start(), calls=%async_computation.1 | async-start | bytes 2359296 | tf_op jit(solution)/shard_map/all_gather | solution.py:107
  8.7 86.3 %all-gather.11.cloned.1.call-start = ((), (), s32[]{:S(2)}) async-start(), calls=%async_computation.3 | async-start | bytes 1179648 | tf_op jit(solution)/shard_map/all_gather | solution.py:111
  9.4 108.9 %all-gather.9.cloned.1.call-start = ((), (), s32[]{:S(2)}) async-start(), calls=%async_computation.2 | async-start | bytes 1179648 | tf_op jit(solution)/shard_map/all_gather | solution.py:110
  10.0 8.6 %copy-start.3 = (bf16[2,64,1024]{2,1,0:T(8,128)(2,1)S(1)}, bf16[2,64,1024]{2,1,0:T(8,128)(2,1)}, u32[]{:S(2)}) copy-start(bf16[2,64,1024]{2,1,0:T(8,128)(2,1)} %param.13) | copy-start | bytes 786436
  84.9 2.3 %copy-start.1 = (bf16[2,32,8,8,512]{4,1,3,2,0:T(8,128)(2,1)S(1)}, bf16[2,32,8,8,512]{4,1,3,2,0:T(8,128)(2,1)}, u32[]{:S(2)}) copy-start(bf16[2,32,8,8,512]{4,1,3,2,0:T(8,128)(2,1)} %get-tuple-element.252) | copy-start | bytes 12582916 | tf_op jit(solution)/shard_map/while/body/eval_jaxpr/cond
  121.3 4.1 %copy-start.2 = (bf16[2,256,1024]{2,1,0:T(8,128)(2,1)S(1)}, bf16[2,256,1024]{2,1,0:T(8,128)(2,1)}, u32[]{:S(2)}) copy-start(bf16[2,256,1024]{2,1,0:T(8,128)(2,1)} %get-tuple-element.235) | copy-start | bytes 3145732 | tf_op jit(solution)/shard_map/while/body/eval_jaxpr/cond
  125.4 1.6 %copy-start = (bf16[2,32,8,8,256]{4,1,3,2,0:T(8,128)(2,1)S(1)}, bf16[2,32,8,8,256]{4,1,3,2,0:T(8,128)(2,1)}, u32[]{:S(2)}) copy-start(bf16[2,32,8,8,256]{4,1,3,2,0:T(8,128)(2,1)} %get-tuple-element.256) | copy-start | bytes 6291460 | tf_op jit(solution)/shard_map/while/body/eval_jaxpr/cond
Sparse Core Ops, SparseCore 0:
  9.6 31.8 all-gather.4
  43.1 28.5 all-gather.6
  73.3 21.6 all-gather.10
  96.4 21.8 all-gather.8
where the time goes:
time: 139 us
  waiting for transfers between devices  81.8 us (59%)
  other arithmetic  16.4 us (12%)
  local copies, waits for them, and re-layouts  15.9 us (11%)
  between operations  15.2 us (11%)
  matrix products  9.3 us (7%)
    all_gather x1, waiting for transfers between devices, on_device(): lax.all_gather(cache_values, 'seq', axis=1, tiled=True)  30.2 us
    all_gather x1, waiting for transfers between devices, on_device(): lax.all_gather(stretch_keys, 'seq', axis=1, tiled=True)  23.3 us
    all_gather x1, waiting for transfers between devices, on_device(): lax.all_gather(cache_keys, 'seq', axis=1, tiled=True)  21.4 us
    cond x11, local copies, waits for them, and re-layouts  9.53 us
    convert_element_type x2, other arithmetic, compute(): weights.astype(jnp.bfloat16)  6.11 us
    dot_general x2, matrix products, compute(): jnp.einsum('srhgk,skhd->srhgd', weights.astype(jnp.bfloat16), value_part,...  5.48 us
    all_gather x1, waiting for transfers between devices, on_device(): lax.all_gather(stretch_values, 'seq', axis=1, tiled=True)  4.29 us
    dot_general x2, matrix products, compute(): jnp.einsum('srhgd,skhd->srhgk', shaped_query, key_part, preferred_element...  3.81 us
  transfers between devices with their start and end apart: 4, of which 4 were waited for; matrix products, arithmetic and copies ran while one was open for 18% of the time, Pallas kernels for 0%

commit v1 on v0

--- a/solution.py
+++ b/solution.py
@@ -3,6 +3,7 @@
 import jax.numpy as jnp
 from jax import lax
 from jax.sharding import PartitionSpec as P
+from jax.lax import all_to_all, axis_size
 
 HQ = 64
 HK = 8
@@ -106,8 +107,21 @@
         lax.all_gather(cache_keys, "seq", axis=1, tiled=True),
         lax.all_gather(cache_values, "seq", axis=1, tiled=True),
     )
+
+    def show_files(field):
+        block_now = jnp.concatenate(
+            all_to_all(
+                jnp.stack(axis_size("seq") * [field], axis=0),
+                axis_name="seq",
+                concat_axis=0,
+                split_axis=0,
+            ),
+            axis=1,
+        )
+        return block_now
+
     new_keys, new_values = (
-        lax.all_gather(stretch_keys, "seq", axis=1, tiled=True),
+        show_files(stretch_keys),
         lax.all_gather(stretch_values, "seq", axis=1, tiled=True),
     )
     old_count = old_keys.shape[1]

time: 139 us -> 132 us (0.950)
  waiting for transfers between devices: 81.8 us -> 69.3 us
  starting transfers between devices: 0.15 us -> 6.6 us
  other arithmetic: 16.4 us -> 13.4 us
    all_gather x1 -> x0, waiting for transfers between devices: 23.3 us -> none  [on_device(): lax.all_gather(stretch_keys, 'seq', axis=1, tiled=True)]
    all_gather x1, waiting for transfers between devices: 21.4 us -> 33.5 us  [on_device(): lax.all_gather(cache_keys, 'seq', axis=1, tiled=True)]
    all_to_all x0 -> x1, starting transfers between devices: none -> 6.49 us  [show_files(): all_to_all(jnp.stack(axis_size('seq') * [field], axis=0), axis_name='seq'...]
    add x2, other arithmetic: 3 us -> 0.08 us  [compute(): new_sum = running_sum * shrink + jnp.sum(weights, axis=-1)]
    another operation x0 -> x2, local copies, waits for them, and re-layouts: none -> 2.1 us  [the longest x1 2.01 us: show_files(): jnp.stack(axis_size('seq') * [field], axis=0)]
    cond x11 -> x15, local copies, waits for them, and re-layouts: 9.53 us -> 10.6 us
  transfers between devices with their start and end apart: 4 -> 4, of which waited for: 4 -> 3; matrix products, arithmetic and copies ran while one was open for 18% -> 19% of each run, Pallas kernels for 0% -> 0%
where the time goes in v1:
time: 132 us; the launch traced here: 131 us
  waiting for transfers between devices  69.3 us (52%)
  local copies, waits for them, and re-layouts  17.2 us (13%)
  between operations  15.2 us (12%)
  other arithmetic  13.4 us (10%)
  matrix products  9.32 us (7%)
  starting transfers between devices  6.6 us (5%)
    all_gather x1, waiting for transfers between devices, on_device(): lax.all_gather(cache_keys, 'seq', axis=1, tiled=True)  33.5 us
    all_gather x1, waiting for transfers between devices, on_device(): lax.all_gather(cache_values, 'seq', axis=1, tiled=True)  29 us
    cond x15, local copies, waits for them, and re-layouts  10.6 us
    all_to_all x1, starting transfers between devices, show_files(): all_to_all(jnp.stack(axis_size('seq') * [field], axis=0), axis_name='seq'...  6.49 us
    convert_element_type x2, other arithmetic, compute(): weights.astype(jnp.bfloat16)  6.11 us
    dot_general x2, matrix products, compute(): jnp.einsum('srhgk,skhd->srhgd', weights.astype(jnp.bfloat16), value_part,...  5.49 us
    all_gather x1, waiting for transfers between devices, on_device(): lax.all_gather(stretch_values, 'seq', axis=1, tiled=True)  4.76 us
    dot_general x2, matrix products, compute(): jnp.einsum('srhgd,skhd->srhgk', shaped_query, key_part, preferred_element...  3.83 us
  transfers between devices with their start and end apart: 4, of which 3 were waited for; matrix products, arithmetic and copies ran while one was open for 19% of the time, Pallas kernels for 0%

profile of v1, /device:TPU:0, one launch (start us, length us, event | category | flops | bytes accessed | tf_op | source)
XLA Modules:
  0.0 131.2 jit_solution(1159934436430674868)
XLA Ops:
  8.7 2.0 %stack.2 = bf16[8,2,32,1024]{3,2,1,0:T(8,128)(2,1)} broadcast(bf16[2,32,1024]{2,1,0:T(8,128)(2,1)} %param.11), dimensions={1,2,3} | broadcast | bytes 1179648 | tf_op jit(solution)/shard_map/stack | solution.py:114
  10.7 6.5 %all-to-all-start = ((bf16[8,2,32,1024]{3,2,1,0:T(8,128)(2,1)}), bf16[8,2,32,1024]{3,2,1,0:T(8,128)(2,1)S(1)}, u32[]{:S(2)}, u32[]{:S(2)}) async-start(bf16[8,2,32,1024]{3,2,1,0:T(8,128)(2,1)} %stack.2), calls=%async_computation | async-start | bytes 2097152 | tf_op jit(solution)/shard_map/all_to_all | solution.py:113
  17.9 1.3 copy.66
  19.8 1.3 fusion.28
  22.4 1.3 compare_reduce_fusion
  24.6 1.0 bitcast_reduce_fusion.3
  27.1 33.5 %all-gather.4.cloned.1.call-done = bf16[2,512,1024]{2,1,0:T(8,128)(2,1)} async-done(((bf16[2,64,1024]{2,1,0:T(8,128)(2,1)}), bf16[2,512,1024]{2,1,0:T(8,128)(2,1)}) %all-gather.4.cloned.1.call-update) | async-done | bytes 2097168 | tf_op jit(solution)/shard_map/all_gather | solution.py:107
  60.6 29.0 %all-gather.6.cloned.1.call-done = bf16[2,512,1024]{2,1,0:T(8,128)(2,1)} async-done(((bf16[2,64,1024]{2,1,0:T(8,128)(2,1)}), bf16[2,512,1024]{2,1,0:T(8,128)(2,1)}) %all-gather.6.cloned.1.call-update) | async-done | bytes 2097168 | tf_op jit(solution)/shard_map/all_gather | solution.py:108
  89.6 18.5 %conditional.2 = ((f32[2,32,8,8]{1,3,2,0:T(8,128)S(1)}, f32[2,32,8,8]{1,3,2,0:T(8,128)S(1)}, f32[2,32,8,8,128]{4,3,1,2,0:T(8,128)S(1)})) conditional(s32[]{:T(128)} %convert_element_type.24, (f32[2,32,8,8]{1,3,2,0:T(8,128)S(1)}, f32[2,32,8,8]{1,3,2,0:T(8,128)S(1)}, f32[2,32,8,8,128]{4,3,1,2,0:T(8,128)S(1)}) %tuple.36, (s32[512]{0:T(512)S(1)}, ...), branch_computations={%region_4.5_spmd, %region_5.8_spmd} | conditional | flops 1091576832 | bytes 72701056 | solution.py:66
  89.6 2.2 %copy.62 = bf16[128,8,8,128]{3,2,1,0:T(8,128)(2,1)S(1)} copy(bf16[128,8,8,128]{3,1,2,0:T(8,128)(2,1)} %bitcast.86) | data formatting | bytes 4194304 | tf_op jit(solution)/shard_map/while/body/eval_jaxpr/cond
  92.0 1.1 copy-done.3
  93.1 2.5 %fusion = (f32[2,32,8,8]{1,3,2,0:T(8,128)S(1)}, f32[2,8,512,32,8]{2,3,4,1,0:T(8,128)S(1)}) fusion(pred[2,512]{1,0:T(4,128)(4,1)S(1)} %broadcast_compare_fusion, bf16[2,32,8,8,128]{4,3,2,1,0:T(8,128)(2,1)S(1)} %copy-done.3, bf16[2,512,8,128,1]{3,2,1,0,4:T(8,128)(2,1)S(1)} %bitcast_bitcast_fusion.1), kind=kOutput, calls=%fused_computation.2 | convolution fusion | flops 543158272 | bytes 11551744 | tf_op jit(solution)/shard_map/while/body/eval_jaxpr/cond/branch_1_fun/srhgd,skhd->srhgk/dot_general | solution.py:42
  95.6 3.6 %fusion.3 = (bf16[2,32,8,8,512]{4,1,3,2,0:T(8,128)(2,1)}, f32[2,32,8,8]{1,3,2,0:T(8,128)S(1)}) fusion(f32[2,8,512,32,8]{2,3,4,1,0:T(8,128)S(1)} %get-tuple-element.273, f32[2,32,8,8]{1,3,2,0:T(8,128)S(1)} %max.7, pred[2,512]{1,0:T(4,128)(4,1)S(1)} %broadcast_compare_fusion), kind=kLoop, calls=%fused_computation.5 | loop fusion | flops 10481664 | bytes 12616704 | tf_op jit(solution)/shard_map/while/body/eval_jaxpr/cond/branch_1_fun/convert_element_type | solution.py:59
  100.1 2.3 %copy.63 = bf16[128,8,8,128]{3,2,1,0:T(8,128)(2,1)S(1)} copy(bf16[128,8,8,128]{3,1,2,0:T(8,128)(2,1)} %bitcast.87) | data formatting | bytes 4194304 | tf_op jit(solution)/shard_map/while/body/eval_jaxpr/cond
  102.5 2.1 %copy-done.1 = bf16[2,32,8,8,512]{4,1,3,2,0:T(8,128)(2,1)S(1)} copy-done((bf16[2,32,8,8,512]{4,1,3,2,0:T(8,128)(2,1)S(1)}, bf16[2,32,8,8,512]{4,1,3,2,0:T(8,128)(2,1)}, u32[]{:S(2)}) %copy-start.1) | copy-done | bytes 4194328 | tf_op jit(solution)/shard_map/while/body/eval_jaxpr/cond
  104.6 3.5 %bitcast_add_fusion = f32[2,32,8,8,128]{4,3,1,2,0:T(8,128)S(1)} fusion(f32[2,32,8,8,128]{4,3,1,2,0:T(8,128)S(1)} %get-tuple-element.185, bf16[2,512,8,128,1]{3,2,1,0,4:T(8,128)(2,1)S(1)} %bitcast_bitcast_fusion, bf16[2,32,8,8,512]{4,1,3,2,0:T(8,128)(2,1)S(1)} %copy-done.1, f32[2,32,8,8]{3,1,2,0:T(8,128)S(1)} %copy-done.6), kind=kOutput, calls=%fused_computation.11 | convolution fusion | flops 537919488 | bytes 10502144 | tf_op jit(solution)/shard_map/while/body/eval_jaxpr/cond/branch_1_fun/srhgk,skhd->srhgd/dot_general | solution.py:57
  108.1 4.8 %all-gather.8.cloned.1.call-done = bf16[2,256,1024]{2,1,0:T(8,128)(2,1)} async-done(((bf16[2,32,1024]{2,1,0:T(8,128)(2,1)}), bf16[2,256,1024]{2,1,0:T(8,128)(2,1)}) %all-gather.8.cloned.1.call-update) | async-done | bytes 1048592 | tf_op jit(solution)/shard_map/all_gather | solution.py:125
  112.8 9.4 %conditional.3 = ((f32[2,32,8,8]{1,3,2,0:T(8,128)S(1)}, f32[2,32,8,8,128]{4,3,1,2,0:T(8,128)S(1)})) conditional(s32[]{:T(128)} %convert_element_type.23, (f32[2,32,8,8]{1,3,2,0:T(8,128)S(1)}, f32[2,32,8,8,128]{4,3,1,2,0:T(8,128)S(1)}) %tuple.38, (s32[256]{0:T(256)S(1)}, s32[32]{0:T(128)S(1)}, bf16[2,8,32,1024]{3,2,0,1:T(8,128)(2,1)S(1)}, ...), branch_computations={%region_8.9_spmd, %region_9.12_spmd.clone} | conditional | flops 546324480 | bytes 43263184 | solution.py:66
  113.4 0.9 copy-done.4
  114.3 1.3 %fusion.15 = (f32[2,32,8,8]{1,3,2,0:T(8,128)S(1)}, f32[2,8,256,32,8]{2,3,4,1,0:T(8,128)S(1)}) fusion(pred[32,256]{1,0:T(8,128)(4,1)S(1)} %broadcast_compare_fusion.1, bf16[2,32,8,8,128]{4,3,2,1,0:T(8,128)(2,1)S(1)} %copy-done.4, bf16[2,256,8,128,1]{3,2,1,0,4:T(8,128)(2,1)S(1)} %bitcast_bitcast_fusion.3), kind=kOutput, calls=%fused_computation.21 | convolution fusion | flops 271577088 | bytes 6316032 | tf_op jit(solution)/shard_map/while/body/eval_jaxpr/cond/branch_1_fun/srhgd,skhd->srhgk/dot_general | solution.py:42
  115.6 2.5 %fusion.18 = (bf16[2,32,8,8,256]{4,1,3,2,0:T(8,128)(2,1)}, f32[2,32,8,8]{1,3,2,0:T(8,128)S(1)}) fusion(f32[2,8,256,32,8]{2,3,4,1,0:T(8,128)S(1)} %get-tuple-element.277, f32[2,32,8,8]{1,3,2,0:T(8,128)S(1)} %max.9, pred[32,256]{1,0:T(8,128)(4,1)S(1)} %broadcast_compare_fusion.1), kind=kLoop, calls=%fused_computation.24 | loop fusion | flops 5238784 | bytes 6332416 | tf_op jit(solution)/shard_map/while/body/eval_jaxpr/cond/branch_1_fun/convert_element_type | solution.py:59
  118.3 1.6 %copy.65 = bf16[64,8,8,128]{3,2,1,0:T(8,128)(2,1)S(1)} copy(bf16[64,8,8,128]{3,1,2,0:T(8,128)(2,1)} %bitcast.89) | data formatting | bytes 2097152 | tf_op jit(solution)/shard_map/while/body/eval_jaxpr/cond
  120.2 2.0 %bitcast_add_fusion.1 = f32[2,32,8,8,128]{4,3,1,2,0:T(8,128)S(1)} fusion(f32[2,32,8,8,128]{4,3,1,2,0:T(8,128)S(1)} %get-tuple-element.252, bf16[2,32,8,8,256]{4,1,3,2,0:T(8,128)(2,1)S(1)} %copy-done, bf16[2,256,8,128,1]{3,2,1,0,4:T(8,128)(2,1)S(1)} %bitcast_bitcast_fusion.2, f32[2,32,8,8]{3,1,2,0:T(8,128)S(1)} %copy.56), kind=kOutput, calls=%fused_computation.26 | convolution fusion | flops 269484032 | bytes 7356416 | tf_op jit(solution)/shard_map/while/body/eval_jaxpr/cond/branch_1_fun/srhgk,skhd->srhgd/dot_general | solution.py:57
  123.4 1.3 convert_element_type.26
  (51 shorter events, 8.5 us)
Async XLA Ops:
  7.2 10.7 %copy-start.2 = (bf16[2,32,8192]{2,1,0:T(8,128)(2,1)S(1)}, bf16[2,32,8192]{2,1,0:T(8,128)(2,1)}, u32[]{:S(2)}) copy-start(bf16[2,32,8192]{2,1,0:T(8,128)(2,1)} %param.10) | copy-start | bytes 3145732
  7.2 53.4 %all-gather.4.cloned.1.call-start = ((), (), s32[]{:S(2)}) async-start(), calls=%async_computation.1 | async-start | bytes 2359296 | tf_op jit(solution)/shard_map/all_gather | solution.py:107
  7.9 81.7 %all-gather.6.cloned.1.call-start = ((), (), s32[]{:S(2)}) async-start(), calls=%async_computation.2 | async-start | bytes 2359296 | tf_op jit(solution)/shard_map/all_gather | solution.py:108
  10.7 8.5 %copy-start.7 = (s32[2]{0:T(128)S(1)}, s32[2]{0:T(128)}, u32[]{:S(2)}) copy-start(s32[2]{0:T(128)} %param.15) | copy-start | bytes 28
  10.7 97.4 %all-to-all-start = ((bf16[8,2,32,1024]{3,2,1,0:T(8,128)(2,1)}), bf16[8,2,32,1024]{3,2,1,0:T(8,128)(2,1)S(1)}, u32[]{:S(2)}, u32[]{:S(2)}) async-start(bf16[8,2,32,1024]{3,2,1,0:T(8,128)(2,1)} %stack.2), calls=%async_computation | async-start | bytes 2097152 | tf_op jit(solution)/shard_map/all_to_all | solution.py:113
  17.2 95.7 %all-gather.8.cloned.1.call-start = ((), (), s32[]{:S(2)}) async-start(), calls=%async_computation.3 | async-start | bytes 1179648 | tf_op jit(solution)/shard_map/all_gather | solution.py:125
  17.9 7.7 %copy-start.5 = (bf16[2,64,1024]{2,1,0:T(8,128)(2,1)S(1)}, bf16[2,64,1024]{2,1,0:T(8,128)(2,1)}, u32[]{:S(2)}) copy-start(bf16[2,64,1024]{2,1,0:T(8,128)(2,1)} %param.13) | copy-start | bytes 786436
  91.9 1.2 copy-start.3
  100.1 2.4 %copy-start.6 = (f32[2,32,8,8]{3,1,2,0:T(8,128)S(1)}, f32[2,32,8,8]{3,1,2,0:T(8,128)}, u32[]{:S(2)}) copy-start(f32[2,32,8,8]{3,1,2,0:T(8,128)} %copy.32) | copy-start | bytes 49156 | tf_op jit(solution)/shard_map/while/body/eval_jaxpr/cond
  102.4 2.2 %copy-start.1 = (bf16[2,32,8,8,512]{4,1,3,2,0:T(8,128)(2,1)S(1)}, bf16[2,32,8,8,512]{4,1,3,2,0:T(8,128)(2,1)}, u32[]{:S(2)}) copy-start(bf16[2,32,8,8,512]{4,1,3,2,0:T(8,128)(2,1)} %get-tuple-element.270) | copy-start | bytes 12582916 | tf_op jit(solution)/shard_map/while/body/eval_jaxpr/cond
  113.0 1.2 copy-start.4
  118.3 1.9 %copy-start = (bf16[2,32,8,8,256]{4,1,3,2,0:T(8,128)(2,1)S(1)}, bf16[2,32,8,8,256]{4,1,3,2,0:T(8,128)(2,1)}, u32[]{:S(2)}) copy-start(bf16[2,32,8,8,256]{4,1,3,2,0:T(8,128)(2,1)} %get-tuple-element.274) | copy-start | bytes 6291460 | tf_op jit(solution)/shard_map/while/body/eval_jaxpr/cond
Sparse Core Ops, SparseCore 0:
  9.6 50.9 all-gather.3
  62.2 27.3 all-gather.5
  91.2 21.6 all-gather.7
